TPU v7x, 256 devices: a whole 4x4x8 slice. The times are simulated.
256 devices in a mesh: row: 4 (over x_hi, core), col: 4 (over y), pt: 16 (over x_lo, z).
Axes of the slice: x: 4 (x_hi: 2, x_lo: 2; x = x_hi * 2 + x_lo), y: 4, z: 8, core: 2. Of those that a mesh axis runs over, the one named last changes fastest.
Arguments:
- first_factors: int32 [32, 1024, 1024], P('pt', 'row', 'col'), may hold values from 0 to 12288
- second_factors: int32 [32, 1024, 1024], P('pt', 'row', 'col'), may hold values from 0 to 12288
Outputs:
- scaled_product: float32 [45, 1024, 1024], P(None, ('row', 'pt'), 'col')
All inputs are finite; a program needn't handle non-finite values.
Results may differ from a plain program's by a relative error of at most 0.0003.
Values may be sent and summed in bfloat16 or wider, within the bound.
No kernel may reach another device: no remote copies, remote signals or barrier semaphores. Data moves between devices by JAX's collectives and lax.ppermute only.
A program may use at most 64 MiB of HBM per device.

v0:
```python
import jax
import jax.numpy as jnp
import numpy as np
from jax import lax
from jax.sharding import PartitionSpec as P

DEG = 16


modulus = 12289
digit_base = 128


def in_blocks(value, dim, peers):
    before, after = (value.shape[:dim], value.shape[dim + 1 :])
    return jnp.moveaxis(value.reshape(*before, peers, -1, *after), dim, 0)


def in_order(pieces, dim):
    dims = list(pieces.shape[1:])
    dims[dim] *= pieces.shape[0]
    return jnp.moveaxis(pieces, 0, dim).reshape(dims)


def one_exchange(value, axis, axes, splits, concats):
    sizes = [lax.axis_size(a) for a in axes]
    pieces = in_blocks(value, splits[0], sizes[0])
    pieces = jnp.moveaxis(in_blocks(pieces, splits[1] + 1, sizes[1]), 0, 1)
    inside = pieces.shape[2:]
    pieces = pieces.reshape(-1, *inside)
    pieces = lax.all_to_all(pieces, axis, split_axis=0, concat_axis=0, tiled=True)
    pieces = in_order(pieces.reshape(*sizes, *inside), concats[0] + 1)
    return in_order(pieces, concats[1])


def in_one_piece(arrays, axis, split_dim, concat_dim, along):
    widths = [a.shape[along] for a in arrays]
    both = jnp.concatenate(arrays, axis=along)
    result = lax.all_to_all(both, axis, split_axis=split_dim, concat_axis=concat_dim, tiled=True)
    return tuple(jnp.split(result, [sum(widths[:k]) for k in range(1, len(widths))], axis=along))


def primitive_root():
    for candidate in range(2, modulus):
        if pow(candidate, 6144, modulus) != 1 and pow(candidate, 4096, modulus) != 1:
            return candidate
    return 0


def make_table(order_size, row_count, column_count, inverse):
    generator = primitive_root()
    root_value = pow(generator, (modulus - 1) // order_size, modulus)
    scaling = 1
    if inverse:
        root_value = pow(root_value, modulus - 2, modulus)
        scaling = pow(order_size, modulus - 2, modulus)
    entries = [
        [
            pow(root_value, row_index * column_index % order_size, modulus) * scaling % modulus
            for column_index in range(column_count)
        ]
        for row_index in range(row_count)
    ]
    return np.array(entries, dtype=np.int64)


def value_digits(values):
    high_digit = values // digit_base
    return (
        high_digit.astype(jnp.bfloat16),
        (values - digit_base * high_digit).astype(jnp.bfloat16),
    )


def combine(high_high, high_low, low_high, low_low):
    top_part = high_high.astype(jnp.int32) % modulus
    middle_part = (high_low.astype(jnp.int32) + low_high.astype(jnp.int32)) % modulus
    return (
        top_part * (digit_base * digit_base) % modulus
        + middle_part * digit_base
        + low_low.astype(jnp.int32)
    ) % modulus


def transform(matrix_table, coefs):
    slot_count = coefs.shape[0]
    flat_coefs = coefs.reshape(slot_count, -1)
    table_high = jnp.asarray(matrix_table // digit_base, dtype=jnp.bfloat16)
    table_low = jnp.asarray(matrix_table % digit_base, dtype=jnp.bfloat16)
    data_high, data_low = value_digits(flat_coefs)

    def product_of(left_part, right_part):
        return jnp.dot(left_part, right_part, preferred_element_type=jnp.float32)

    mixed_values = combine(
        product_of(table_high, data_high),
        product_of(table_high, data_low),
        product_of(table_low, data_high),
        product_of(table_low, data_low),
    )
    return mixed_values.reshape(matrix_table.shape[0], coefs.shape[1], coefs.shape[2])


def batched_product(left_part, right_part):
    return jnp.einsum("bik,bkj->bij", left_part, right_part, preferred_element_type=jnp.float32)


def digit_sum(totals, left_digits, right_digits):
    return (
        totals[0] + batched_product(left_digits[0], right_digits[0]),
        totals[1] + batched_product(left_digits[0], right_digits[1]),
        totals[2] + batched_product(left_digits[1], right_digits[0]),
        totals[3] + batched_product(left_digits[1], right_digits[1]),
    )


def pointwise(left_values, right_values):
    left_points, right_points = (
        one_exchange(left_values.astype(jnp.float32), ("col", "pt"), ("col", "pt"), (0, 0), (2, 1)),
        one_exchange(
            right_values.astype(jnp.float32), ("col", "pt"), ("col", "pt"), (0, 0), (2, 1)
        ),
    )
    left_digits = value_digits(left_points.astype(jnp.int32))
    right_digits = value_digits(right_points.astype(jnp.int32))
    zeros_init = jnp.zeros(left_points.shape, jnp.float32)
    column_parts = tuple((digit_part for digit_part in left_digits))
    totals = digit_sum(
        (zeros_init, zeros_init, zeros_init, zeros_init),
        column_parts,
        (
            lax.all_gather(right_digits[0], "row", axis=1, tiled=True),
            lax.all_gather(right_digits[1], "row", axis=1, tiled=True),
        ),
    )
    product_values = combine(totals[0], totals[1], totals[2], totals[3]).astype(jnp.float32)
    arrived = one_exchange(product_values, ("col", "pt"), ("col", "pt"), (2, 1), (0, 0))
    col_count = lax.axis_size("col")
    pt_count = lax.axis_size("pt")
    local_count = arrived.shape[0] // (col_count * pt_count)
    returned = arrived.reshape(pt_count, col_count, local_count, arrived.shape[1], arrived.shape[2])
    returned = returned.transpose(1, 0, 2, 3, 4).reshape(arrived.shape)
    return returned.astype(jnp.int32)


def local(first_factors, second_factors):
    forward_one = make_table(2 * DEG, 2 * DEG, DEG, False)
    inverse_one = make_table(2 * DEG, 2 * DEG, 2 * DEG, True)
    forward_two = make_table(4 * DEG, 4 * DEG, 2 * DEG, False)
    inverse_two = make_table(4 * DEG, 3 * DEG - 3, 4 * DEG, True)
    first_entries, second_entries = in_one_piece(
        (first_factors.astype(jnp.float32), second_factors.astype(jnp.float32)), "pt", 1, 0, 2
    )
    first_entries = first_entries.astype(jnp.int32)
    second_entries = second_entries.astype(jnp.int32)
    left_values = jnp.concatenate(
        [transform(forward_one, first_entries[:DEG]), transform(forward_one, first_entries[DEG:])],
        0,
    )
    right_values = jnp.concatenate(
        [
            transform(forward_one, second_entries[:DEG]),
            transform(forward_one, second_entries[DEG:]),
        ],
        0,
    )
    products = pointwise(left_values, right_values)
    first_product = transform(inverse_one, products[: 2 * DEG])
    second_product = transform(inverse_one, products[2 * DEG :])
    upper_values = transform(forward_two, first_product)
    lower_values = transform(forward_two[:, :DEG], second_product[DEG:])
    result_coefficients = transform(inverse_two, pointwise(upper_values, lower_values))
    return result_coefficients.astype(jnp.float32) / 12289.0


def solution(mesh):
    in_specs = (P("pt", "row", "col"), P("pt", "row", "col"))
    out_specs = P(None, ("row", "pt"), "col")
    return jax.shard_map(local, mesh=mesh, in_specs=in_specs, out_specs=out_specs, check_vma=False)
```

profile of v0, /device:TPU:32, one launch (start us, length us, event | category | flops | bytes accessed | tf_op | source)
XLA Modules:
  0.0 372.5 jit_solution(14811177652636000690)
XLA Ops:
  6.5 1.1 convert_element_type.505
  7.6 1.1 convert_element_type.506
  8.8 0.8 copy.57
  9.6 35.5 %all_to_all.48 = f32[2,256,512]{2,0,1:T(2,128)S(1)} all-to-all(f32[2,256,512]{2,0,1:T(2,128)S(1)} %copy.57), channel_id=1, replica_groups=mesh['row'=4,'col'=4,'pt'=16] {'pt'}, dimensions={1} | all-to-all | bytes 2097152 | tf_op jit(solution)/shard_map/all_to_all | solution.py:39
  48.0 1.0 add_select_fusion.35
  49.6 1.0 add_select_fusion.39
  50.9 37.4 %all_to_all.49 = f32[64,1,16,256]{3,2,1,0:T(8,128)S(1)} all-to-all(f32[64,1,16,256]{3,2,1,0:T(8,128)S(1)} %add_convert_fusion.1), channel_id=1, replica_groups=mesh['row'=4,'col'=4,'pt'=16] {'col','pt'}, dimensions={0} | all-to-all | bytes 2097152 | tf_op jit(solution)/shard_map/all_to_all | solution.py:31
  88.5 0.7 copy.66
  89.7 1.7 fusion.181
  92.9 1.0 add_select_fusion.47
  95.2 1.0 add_select_fusion.43
  96.4 1.1 add_convert_fusion
  97.5 5.7 %all-to-all-start.1 = ((f32[64,1,16,256]{3,2,1,0:T(8,128)}), f32[64,1,16,256]{3,2,1,0:T(8,128)S(1)}, u32[]{:S(2)}, u32[]{:S(2)}) async-start(f32[64,1,16,256]{3,2,1,0:T(8,128)} %add_convert_fusion), calls=%async_computation.1 | async-start | bytes 2097152 | tf_op jit(solution)/shard_map/all_to_all | solution.py:31
  103.3 0.7 all-gather.7.cloned.1.call-update
  104.3 27.2 %all-to-all-done.1 = f32[64,1,16,256]{3,2,1,0:T(8,128)S(1)} async-done(((f32[64,1,16,256]{3,2,1,0:T(8,128)}), f32[64,1,16,256]{3,2,1,0:T(8,128)S(1)}, u32[]{:S(2)}, u32[]{:S(2)}) %all-to-all-start.1) | async-done | bytes 1048608 | tf_op jit(solution)/shard_map/all_to_all | solution.py:31
  131.7 0.7 fusion.180
  133.5 2.4 fusion.89
  135.9 1.0 fusion.137
  137.0 21.1 %all-gather.7.cloned.1.call-done = bf16[1,1024,1024]{2,1,0:T(8,128)(2,1)} async-done(((bf16[1,256,1024]{2,1,0:T(8,128)(2,1)}), bf16[1,1024,1024]{2,1,0:T(8,128)(2,1)}) %all-gather.7.cloned.1.call-update) | async-done | bytes 2097168 | tf_op jit(solution)/shard_map/all_gather | solution.py:133
  158.1 2.8 fusion.134
  160.8 3.3 fusion.146
  164.9 39.5 %all_to_all.50 = f32[64,1,16,256]{3,2,1,0:T(8,128)S(1)} all-to-all(f32[64,1,16,256]{3,2,1,0:T(8,128)S(1)} %bitcast.333), channel_id=1, replica_groups=mesh['row'=4,'col'=4,'pt'=16] {'col','pt'}, dimensions={0} | all-to-all | bytes 2097152 | tf_op jit(solution)/shard_map/all_to_all | solution.py:31
  205.3 1.0 add_select_fusion.26
  206.8 0.7 fusion.210
  209.2 1.9 fusion.157
  211.4 34.7 %all_to_all.51 = f32[64,1,16,256]{3,2,1,0:T(8,128)S(1)} all-to-all(f32[64,1,16,256]{3,2,1,0:T(8,128)S(1)} %bitcast.334), channel_id=1, replica_groups=mesh['row'=4,'col'=4,'pt'=16] {'col','pt'}, dimensions={0} | all-to-all | bytes 2097152 | tf_op jit(solution)/shard_map/all_to_all | solution.py:31
  246.3 0.7 copy.74
  247.6 1.7 fusion.183
  251.3 1.2 add_select_fusion.30
  252.6 0.9 fusion.3
  254.0 0.9 fusion.6
  254.9 2.2 fusion.151
  257.1 1.3 copy.89
  258.4 5.7 %all-to-all-start.4 = ((f32[64,1,16,256]{3,2,1,0:T(8,128)}), f32[64,1,16,256]{3,2,1,0:T(8,128)S(1)}, u32[]{:S(2)}, u32[]{:S(2)}) async-start(f32[64,1,16,256]{3,2,1,0:T(8,128)} %bitcast.36), calls=%async_computation.4 | async-start | bytes 2097152 | tf_op jit(solution)/shard_map/all_to_all | solution.py:31
  264.7 27.7 %all-to-all-done.4 = f32[64,1,16,256]{3,2,1,0:T(8,128)S(1)} async-done(((f32[64,1,16,256]{3,2,1,0:T(8,128)}), f32[64,1,16,256]{3,2,1,0:T(8,128)S(1)}, u32[]{:S(2)}, u32[]{:S(2)}) %all-to-all-start.4) | async-done | bytes 1048608 | tf_op jit(solution)/shard_map/all_to_all | solution.py:31
  292.5 0.7 fusion.182
  294.3 2.6 fusion.101
  296.9 1.0 fusion.122
  297.9 14.5 %all-gather.11.cloned.1.call-done = bf16[1,1024,1024]{2,1,0:T(8,128)(2,1)} async-done(((bf16[1,256,1024]{2,1,0:T(8,128)(2,1)}), bf16[1,1024,1024]{2,1,0:T(8,128)(2,1)}) %all-gather.11.cloned.1.call-update) | async-done | bytes 2097168 | tf_op jit(solution)/shard_map/all_gather | solution.py:133
  312.4 2.8 fusion.119
  315.2 3.3 fusion.163
  319.2 39.5 %all_to_all.52 = f32[64,1,16,256]{3,2,1,0:T(8,128)S(1)} all-to-all(f32[64,1,16,256]{3,2,1,0:T(8,128)S(1)} %bitcast.336), channel_id=1, replica_groups=mesh['row'=4,'col'=4,'pt'=16] {'col','pt'}, dimensions={0} | all-to-all | bytes 2097152 | tf_op jit(solution)/shard_map/all_to_all | solution.py:31
  358.9 0.6 copy.94
  359.5 0.9 convolution_convert_fusion.10
  360.4 1.0 fusion.23
  361.5 1.1 fusion.21
  362.5 2.0 fusion.179
  364.8 0.9 slice.40
  (98 shorter events, 18.7 us)
Async XLA Ops:
  6.5 126.9 %all-gather.5.cloned.1.call-start = ((), (), s32[]{:S(2)}) async-start(), calls=%async_computation.7 | async-start | bytes 2621440 | tf_op jit(solution)/shard_map/all_gather | solution.py:132
  45.4 0.7 copy-start.13
  46.4 1.3 copy-start.12
  97.5 34.0 %all-to-all-start.1 = ((f32[64,1,16,256]{3,2,1,0:T(8,128)}), f32[64,1,16,256]{3,2,1,0:T(8,128)S(1)}, u32[]{:S(2)}, u32[]{:S(2)}) async-start(f32[64,1,16,256]{3,2,1,0:T(8,128)} %add_convert_fusion), calls=%async_computation.1 | async-start | bytes 2097152 | tf_op jit(solution)/shard_map/all_to_all | solution.py:31
  103.3 54.8 %all-gather.7.cloned.1.call-start = ((), (), s32[]{:S(2)}) async-start(), calls=%async_computation.8 | async-start | bytes 2621440 | tf_op jit(solution)/shard_map/all_gather | solution.py:133
  104.0 190.3 %all-gather.9.cloned.1.call-start = ((), (), s32[]{:S(2)}) async-start(), calls=%async_computation.9 | async-start | bytes 2621440 | tf_op jit(solution)/shard_map/all_gather | solution.py:132
  133.5 2.5 copy-start
  158.1 2.8 copy-start.2
  204.5 0.8 copy-start.7
  205.3 1.2 copy-start.6
  206.7 1.1 copy-start.4
  206.7 1.6 copy-start.5
  251.3 1.3 copy-start.9
  252.6 0.9 copy-start.8
  258.4 33.9 %all-to-all-start.4 = ((f32[64,1,16,256]{3,2,1,0:T(8,128)}), f32[64,1,16,256]{3,2,1,0:T(8,128)S(1)}, u32[]{:S(2)}, u32[]{:S(2)}) async-start(f32[64,1,16,256]{3,2,1,0:T(8,128)} %bitcast.36), calls=%async_computation.4 | async-start | bytes 2097152 | tf_op jit(solution)/shard_map/all_to_all | solution.py:31
  264.1 48.3 %all-gather.11.cloned.1.call-start = ((), (), s32[]{:S(2)}) async-start(), calls=%async_computation.10 | async-start | bytes 2621440 | tf_op jit(solution)/shard_map/all_gather | solution.py:133
  294.3 2.6 copy-start.1
  312.4 2.8 copy-start.3
  358.7 0.7 copy-start.11
  360.4 1.1 copy-start.10
Sparse Core Ops, SparseCore 0:
  91.6 34.5 all-gather.4
  128.0 29.9 all-gather.6
  249.4 30.9 all-gather.8
  282.1 30.2 all-gather.10
where the time goes:
time: 378 us; the launch traced here: 372 us
  blocking collectives  187 us (49%)
  waiting for transfers between devices  91.6 us (24%)
  matrix products  45.4 us (12%)
  between operations  14.2 us (4%)
  local copies, waits for them, and re-layouts  12.8 us (3%)
  starting transfers between devices  12 us (3%)
  other arithmetic  9.9 us (3%)
    all_to_all x4, blocking collectives, one_exchange(): lax.all_to_all(pieces, axis, split_axis=0, concat_axis=0, tiled=True)  151 us
    all_to_all x2, waiting for transfers between devices, one_exchange(): lax.all_to_all(pieces, axis, split_axis=0, concat_axis=0, tiled=True)  54.9 us
    all_gather x2, waiting for transfers between devices, pointwise(): lax.all_gather(right_digits[1], 'row', axis=1, tiled=True)  35.6 us
    all_to_all x1, blocking collectives, in_one_piece(): lax.all_to_all(both, axis, split_axis=split_dim, concat_axis=concat_dim,...  35.5 us
    dot_general x36, matrix products, product_of(): return jnp.dot(left_part, right_part, preferred_element_type=jnp.float32)  26.2 us
    dot_general x8, matrix products, batched_product(): jnp.einsum('bik,bkj->bij', left_part, right_part, preferred_element_type=...  19.2 us
    all_to_all x2, starting transfers between devices, one_exchange(): lax.all_to_all(pieces, axis, split_axis=0, concat_axis=0, tiled=True)  11.4 us
  transfers between devices with their start and end apart: 6, of which 4 were waited for; matrix products, arithmetic and copies ran while one was open for 7% of the time, Pallas kernels for 0%

commit v1 on v0

v1 whole, which is shorter than its diff:
```python
import functools

import jax
import jax.numpy as jnp
import numpy as np
from jax import lax
from jax.experimental import pallas as pl
from jax.experimental.pallas import tpu as pltpu
from jax.sharding import PartitionSpec as P

DEG = 16
POINTS = 48
COEFS = 3 * DEG - 3

modulus = 12289
inverse_modulus = 1.0 / modulus


def primitive_root():
    for candidate in range(2, modulus):
        if pow(candidate, 6144, modulus) != 1 and pow(candidate, 4096, modulus) != 1:
            return candidate
    return 0


def powers(order, row_count, column_count, inverse=False):
    root = pow(primitive_root(), (modulus - 1) // order, modulus)
    scaling = 1
    if inverse:
        root = pow(root, modulus - 2, modulus)
        scaling = pow(order, modulus - 2, modulus)
    entries = [
        [pow(root, i * j % order, modulus) * scaling % modulus for j in range(column_count)]
        for i in range(row_count)
    ]
    return np.array(entries, dtype=np.int64)


def matrix_inverse(matrix):
    size = matrix.shape[0]
    work = np.concatenate([matrix % modulus, np.eye(size, dtype=np.int64)], axis=1)
    for k in range(size):
        pivot = k + int(np.nonzero(work[k:, k])[0][0])
        work[[k, pivot]] = work[[pivot, k]]
        work[k] = work[k] * pow(int(work[k, k]), modulus - 2, modulus) % modulus
        for i in range(size):
            if i != k:
                work[i] = (work[i] - work[i, k] * work[k]) % modulus
    return work[:, size:]


def centred(values):
    values = values % modulus
    return np.where(values > modulus // 2, values - modulus, values)


def table_digits(values):
    values = centred(values)
    high = (values + 64) >> 7
    return high, values - 128 * high


def expanded_table(matrix):
    of_high, of_low = table_digits(128 * matrix), table_digits(matrix)
    parts = np.stack([np.stack([of_high[k], of_low[k]], 0) for k in range(2)], 0)
    outputs, inputs = matrix.shape
    full = np.einsum("pdoi,rs->pordis", parts, np.eye(8, dtype=np.int64))
    return jnp.asarray(full.reshape(2 * outputs * 8, 2 * inputs * 8), dtype=jnp.bfloat16)


def reduced(value):
    return value - jnp.floor(value * inverse_modulus + 0.5) * float(modulus)


def mixed(table_ref, slots):
    inputs = slots.shape[0]
    half_rows = table_ref.shape[0] // 2
    outputs = half_rows // 8
    halves = []
    for h in range(2):
        part = slots[:, 8 * h : 8 * h + 8, :].reshape(inputs * 8, 256)
        high = (part + 64) >> 7
        low = part - (high << 7)
        digits = jnp.concatenate(
            [high.astype(jnp.float32).astype(jnp.bfloat16), low.astype(jnp.float32).astype(jnp.bfloat16)], 0
        )
        sums = jnp.dot(table_ref[...], digits, preferred_element_type=jnp.float32)
        top, bottom = sums[:half_rows], sums[half_rows:]
        quotient = jnp.floor(top * (128.0 * inverse_modulus) + bottom * inverse_modulus + 0.5)
        value = (top - 96.0 * quotient) * 128.0 + (bottom - quotient)
        halves.append(value.reshape(outputs, 8, 256))
    return jnp.concatenate(halves, axis=1)


def to_wire(value):
    return value.astype(jnp.int32).astype(jnp.int16)


def pack_kernel(first_ref, second_ref, out_ref):
    for a, ref in enumerate((first_ref, second_ref)):
        for b in range(2):
            out_ref[:, a, b] = ref[b].astype(jnp.int16).reshape(16, 16, 256)


def spread_kernel(table_ref, in_ref, out_ref):
    count = out_ref.shape[1] // 2
    for a in range(2):
        slots = in_ref[:, a].astype(jnp.int32).reshape(16, 16, 256)
        value = to_wire(mixed(table_ref, slots))
        out_ref[:, a * count : (a + 1) * count] = value.reshape(16, count, 16, 256)


def middle_kernel(table_ref, in_ref, out_ref):
    slots = in_ref[...].astype(jnp.int32).reshape(-1, 16, 256)
    out_ref[...] = to_wire(mixed(table_ref, slots)).reshape(out_ref.shape)


def final_kernel(table_ref, in_ref, out_ref):
    slots = in_ref[...].astype(jnp.int32).reshape(-1, 16, 256)
    value = mixed(table_ref, slots)
    value = jnp.where(value < 0.0, value + float(modulus), value)
    out_ref[...] = value / float(modulus)


def product_kernel(shift_ref, *refs):
    left_refs, right_refs, out_ref = refs[:4], refs[4:8], refs[8]
    left_scratch, right_scratch = refs[9:12], refs[12:15]
    shift = shift_ref[0]

    def store_digits(piece, scratch, place):
        value = piece.astype(jnp.int32).reshape(256, 256)
        high = (value + 64) >> 7
        low = value - (high << 7)
        both = high + low
        for part, ref in zip((high, low, both), scratch):
            ref[place] = part.astype(jnp.float32).astype(jnp.bfloat16)

    for j in range(out_ref.shape[1]):
        for m in range(4):
            store_digits(left_refs[m][:, j], left_scratch, (slice(None), slice(256 * m, 256 * m + 256)))
            block = pl.multiple_of((m ^ shift) * 256, 256)
            store_digits(right_refs[m][:, j], right_scratch, (pl.ds(block, 256), slice(None)))
        high_high, low_low, both_both = (
            jnp.dot(left[...], right[...], preferred_element_type=jnp.float32)
            for left, right in zip(left_scratch, right_scratch)
        )
        value = reduced(high_high) * 128.0 + (both_both - high_high - low_low)
        value = reduced(reduced(value) * 128.0 + low_low)
        out_ref[:, j] = to_wire(value).reshape(16, 16, 256)


def whole(shape):
    return pl.BlockSpec(shape, lambda i: (0,) * len(shape))


def params():
    return pltpu.CompilerParams(dimension_semantics=("arbitrary",), vmem_limit_bytes=24 * 1024 * 1024)


def cost(flops):
    return pl.CostEstimate(flops=flops, bytes_accessed=1 << 20, transcendentals=0)


def pack(first, second):
    return pl.pallas_call(
        pack_kernel,
        grid=(1,),
        out_shape=jax.ShapeDtypeStruct((16, 2, 2, 16, 256), jnp.int16),
        in_specs=[whole((2, 256, 256))] * 2,
        out_specs=whole((16, 2, 2, 16, 256)),
        compiler_params=params(),
        cost_estimate=cost(1 << 20),
        name="pack",
    )(first, second)


def spread(table, entries, pair, name):
    count = table.shape[0] // 256
    out_shape = (16, 2 * count, 16, 256)
    return pl.pallas_call(
        spread_kernel,
        grid=(1,),
        out_shape=jax.ShapeDtypeStruct(out_shape, jnp.int16),
        in_specs=[whole(table.shape), pl.BlockSpec((8, 2, 2, 16, 256), lambda i: (pair, 0, 0, 0, 0))],
        out_specs=whole(out_shape),
        compiler_params=params(),
        cost_estimate=cost(4 * 2 * table.shape[0] * table.shape[1] * 256),
        name=name,
    )(table, entries)


def middle(table, values):
    out_shape = (16, POINTS // 16, 16, 256)
    return pl.pallas_call(
        middle_kernel,
        grid=(1,),
        out_shape=jax.ShapeDtypeStruct(out_shape, jnp.int16),
        in_specs=[whole(table.shape), whole(values.shape)],
        out_specs=whole(out_shape),
        compiler_params=params(),
        cost_estimate=cost(2 * 2 * table.shape[0] * table.shape[1] * 256),
        name="middle",
    )(table, values)


def final(table, values):
    out_shape = (COEFS, 16, 256)
    return pl.pallas_call(
        final_kernel,
        grid=(1,),
        out_shape=jax.ShapeDtypeStruct(out_shape, jnp.float32),
        in_specs=[whole(table.shape), whole(values.shape)],
        out_specs=whole(out_shape),
        compiler_params=params(),
        cost_estimate=cost(2 * 2 * table.shape[0] * table.shape[1] * 256),
        name="final",
    )(table, values)


def product(shift, left, right, name):
    shape = left[0].shape
    return pl.pallas_call(
        product_kernel,
        grid=(1,),
        out_shape=jax.ShapeDtypeStruct(shape, jnp.int16),
        in_specs=[pl.BlockSpec(memory_space=pltpu.SMEM)] + [whole(shape)] * 8,
        out_specs=whole(shape),
        scratch_shapes=[pltpu.VMEM((256, 1024), jnp.bfloat16)] * 3 + [pltpu.VMEM((1024, 256), jnp.bfloat16)] * 3,
        compiler_params=params(),
        cost_estimate=cost(shape[1] * 3 * 2 * 256 * 256 * 1024),
        name=name,
    )(shift, *left, *right)


def exchange(value):
    return lax.all_to_all(value, "pt", split_axis=0, concat_axis=0, tiled=True)


def swapped(value, axis, bits):
    return lax.ppermute(value, axis, [(i, i ^ bits) for i in range(4)])


def along_columns(value):
    return [value] + [swapped(value, "col", m) for m in (1, 2, 3)]


def along_rows(value):
    across = swapped(value, "row", 2)
    return [value, swapped(value, "row", 1), across, swapped(across, "row", 1)]


def local(first_factors, second_factors):
    forward_two = powers(4 * DEG, POINTS, 2 * DEG)
    spread_one = expanded_table(powers(2 * DEG, 2 * DEG, DEG))
    spread_two = expanded_table(forward_two[:, :DEG])
    lift = forward_two[:, :DEG] @ powers(2 * DEG, 2 * DEG, 2 * DEG, True)[DEG:] % modulus
    back = matrix_inverse(powers(4 * DEG, POINTS, POINTS))[:COEFS]
    shift = (lax.axis_index("row") ^ lax.axis_index("col")).astype(jnp.int32).reshape(1)

    entries = exchange(pack(first_factors, second_factors))
    at_one = exchange(spread(spread_one, entries, 1, "spread_one"))
    to_two = spread(spread_two, entries, 0, "spread_two")
    left_one, right_one = along_columns(at_one[:, :2]), along_rows(at_one[:, 2:])
    to_two, at_one = lax.optimization_barrier((to_two, at_one))
    at_two = exchange(to_two)
    products_one = product(shift, left_one, right_one, "product_one")
    products_one, at_two = lax.optimization_barrier((products_one, at_two))
    returned = exchange(products_one)
    left_two, right_two = along_columns(at_two[:, :3]), along_rows(at_two[:, 3:])
    upper = along_columns(product(shift, left_two, right_two, "product_upper"))
    to_lower = middle(expanded_table(lift), returned)
    lower = along_rows(exchange(to_lower))
    products_two = exchange(product(shift, upper_in_rows(upper), lower, "product_two"))
    return final(expanded_table(back), products_two)


def upper_in_rows(upper):
    return upper


def solution(mesh):
    in_specs = (P("pt", "row", "col"), P("pt", "row", "col"))
    out_specs = P(None, ("row", "pt"), "col")
    return jax.shard_map(local, mesh=mesh, in_specs=in_specs, out_specs=out_specs, check_vma=False)
```

time: 378 us -> 168 us (0.44); the launches traced: 372 us -> 167 us
  blocking collectives: 187 us -> 58.6 us
  matrix products: 45.4 us -> 0 us
  waiting for transfers between devices: 91.6 us -> 53 us
  starting transfers between devices: 12 us -> 35.4 us
  Pallas kernels: 0 us -> 16.7 us
  between operations: 14.2 us -> 0.09 us
  other arithmetic: 9.9 us -> 0 us
  local copies, waits for them, and re-layouts: 12.8 us -> 3.3 us
    all_to_all x5 -> x3, blocking collectives: 187 us -> 58.6 us  [exchange(): return lax.all_to_all(value, 'pt', split_axis=0, concat_axis=0, tiled=True)]
    dot_general x44 -> x0, matrix products: 45.4 us -> none  [the longest x36 26.2 us: product_of(): return jnp.dot(left_part, right_part, preferred_element_type=jnp.float32)]
    all_to_all x2 -> x3, waiting for transfers between devices: 54.9 us -> 12.8 us  [exchange(): return lax.all_to_all(value, 'pt', split_axis=0, concat_axis=0, tiled=True)]
    ppermute x0 -> x18, waiting for transfers between devices: none -> 40.3 us  [swapped(): return lax.ppermute(value, axis, [(i, i ^ bits) for i in range(4)])]
    all_gather x4 -> x0, waiting for transfers between devices: 35.6 us -> none  [the longest x2 35.6 us: pointwise(): lax.all_gather(right_digits[1], 'row', axis=1, tiled=True)]
    ppermute x0 -> x18, starting transfers between devices: none -> 20.8 us  [swapped(): return lax.ppermute(value, axis, [(i, i ^ bits) for i in range(4)])]
    pallas_call x0 -> x8, Pallas kernels: none -> 16.7 us  [the longest x3 9.64 us: product(): pl.pallas_call(product_kernel, grid=(1,), out_shape=jax.ShapeDtypeStruct(...]
    convert_element_type x17 -> x0, other arithmetic: 9.79 us -> none  [the longest x5 5.24 us: value_digits(): high_digit.astype(jnp.bfloat16)]
  transfers between devices with their start and end apart: 6 -> 21, of which waited for: 4 -> 11; matrix products, arithmetic and copies ran while one was open for 7% -> 1% of each run, Pallas kernels for 0% -> 5%
where the time goes in v1:
time: 168 us; the launch traced here: 167 us
  blocking collectives  58.6 us (35%)
  waiting for transfers between devices  53 us (32%)
  starting transfers between devices  35.4 us (21%)
  Pallas kernels  16.7 us (10%)
  local copies, waits for them, and re-layouts  3.3 us (2%)
    all_to_all x3, blocking collectives, exchange(): return lax.all_to_all(value, 'pt', split_axis=0, concat_axis=0, tiled=True)  58.6 us
    ppermute x18, waiting for transfers between devices, swapped(): return lax.ppermute(value, axis, [(i, i ^ bits) for i in range(4)])  40.3 us
    ppermute x18, starting transfers between devices, swapped(): return lax.ppermute(value, axis, [(i, i ^ bits) for i in range(4)])  20.8 us
    all_to_all x3, starting transfers between devices, exchange(): return lax.all_to_all(value, 'pt', split_axis=0, concat_axis=0, tiled=True)  14.6 us
    all_to_all x3, waiting for transfers between devices, exchange(): return lax.all_to_all(value, 'pt', split_axis=0, concat_axis=0, tiled=True)  12.8 us
    pallas_call x3, Pallas kernels, product(): pl.pallas_call(product_kernel, grid=(1,), out_shape=jax.ShapeDtypeStruct(...  9.64 us
    pallas_call x2, Pallas kernels, spread(): pl.pallas_call(spread_kernel, grid=(1,), out_shape=jax.ShapeDtypeStruct(o...  3.5 us
  transfers between devices with their start and end apart: 21, of which 11 were waited for; matrix products, arithmetic and copies ran while one was open for 1% of the time, Pallas kernels for 5%

profile of v1, /device:TPU:32, one launch (start us, length us, event | category | flops | bytes accessed | tf_op | source)
XLA Modules:
  0.0 167.1 jit_solution(15127526159480327148)
XLA Ops:
  0.0 1.0 copy-done.1
  1.0 1.0 copy-done.2
  2.1 0.1 pack.1
  2.1 24.4 %all_to_all.30.in_ref = s16[16,2,2,16,256]{4,3,2,1,0:T(8,128)(2,1)S(1)} all-to-all(s16[16,2,2,16,256]{4,3,2,1,0:T(8,128)(2,1)S(1)} %pack.1), channel_id=1, replica_groups=mesh['row'=4,'col'=4,'pt'=16] {'pt'}, dimensions={0} | all-to-all | bytes 1048576 | tf_op jit(solution)/shard_map/all_to_all | solution.py:236
  26.6 1.5 spread_one.1
  28.1 5.3 %all-to-all-start.1 = ((s16[16,4,16,256]{3,2,1,0:T(8,128)(2,1)}), s16[16,4,16,256]{3,2,1,0:T(8,128)(2,1)S(1)}, u32[]{:S(2)}, u32[]{:S(2)}) async-start(s16[16,4,16,256]{3,2,1,0:T(8,128)(2,1)} %spread_one.1), calls=%async_computation.1 | async-start | bytes 1048576 | tf_op jit(solution)/shard_map/all_to_all | solution.py:236
  33.4 2.0 %spread_two.1 = s16[16,6,16,256]{3,2,1,0:T(8,128)(2,1)} custom-call(bf16[768,256]{1,0:T(8,128)(2,1)S(1)} %copy-done.3, s16[16,2,2,16,256]{4,3,2,1,0:T(8,128)(2,1)S(1)} %all_to_all.30.in_ref), custom_call_target="tpu_custom_call" | custom-call | flops 402653184 | bytes 1048576 | tf_op jit(solution)/shard_map/spread_two/pallas_call | solution.py:180
  35.4 12.7 %all-to-all-done.1 = s16[16,4,16,256]{3,2,1,0:T(8,128)(2,1)S(1)} async-done(((s16[16,4,16,256]{3,2,1,0:T(8,128)(2,1)}), s16[16,4,16,256]{3,2,1,0:T(8,128)(2,1)S(1)}, u32[]{:S(2)}, u32[]{:S(2)}) %all-to-all-start.1) | async-done | bytes 524320 | tf_op jit(solution)/shard_map/all_to_all | solution.py:236
  48.1 5.2 %all-to-all-start.2 = ((s16[16,6,16,256]{3,2,1,0:T(8,128)(2,1)}), s16[16,6,16,256]{3,2,1,0:T(8,128)(2,1)}, u32[]{:S(2)}, u32[]{:S(2)}) async-start(s16[16,6,16,256]{3,2,1,0:T(8,128)(2,1)} %spread_two.1), calls=%async_computation.2 | async-start | bytes 1572864 | tf_op jit(solution)/shard_map/all_to_all | solution.py:236
  53.3 2.8 %collective-permute-start.4 = (s16[16,2,16,256]{3,2,1,0:T(8,128)(2,1)S(1)}, s16[16,2,16,256]{3,2,1,0:T(8,128)(2,1)S(1)}, u32[]{:S(2)}, u32[]{:S(2)}) collective-permute-start(s16[16,2,16,256]{3,2,1,0:T(8,128)(2,1)S(1)} %get-tuple-element.13.refs_4_), channel_id=1, source_target_pairs={{0,128},{64,192},{128,0},{192,64},{1,129},{65,193},{129,1},{193,65... | collective-permute-start | bytes 786440 | tf_op jit(solution)/shard_map/ppermute | solution.py:240
  56.1 1.6 collective-permute-start
  57.7 2.9 %collective-permute-start.1 = (s16[16,2,16,256]{3,2,1,0:T(8,128)(2,1)S(1)}, s16[16,2,16,256]{3,2,1,0:T(8,128)(2,1)S(1)}, u32[]{:S(2)}, u32[]{:S(2)}) collective-permute-start(s16[16,2,16,256]{3,2,1,0:T(8,128)(2,1)S(1)} %get-tuple-element.14.refs_0_), channel_id=1, source_target_pairs={{0,32},{16,48},{32,0},{48,16},{1,33},{17,49},{33,1},{49,17},{2,34}... | collective-permute-start | bytes 786440 | tf_op jit(solution)/shard_map/ppermute | solution.py:240
  60.6 0.2 collective-permute-start.2
  60.8 0.0 collective-permute-start.3
  60.8 5.3 %collective-permute-done.4.refs_6_ = s16[16,2,16,256]{3,2,1,0:T(8,128)(2,1)S(1)} collective-permute-done((s16[16,2,16,256]{3,2,1,0:T(8,128)(2,1)S(1)}, s16[16,2,16,256]{3,2,1,0:T(8,128)(2,1)S(1)}, u32[]{:S(2)}, u32[]{:S(2)}) %collective-permute-start.4) | collective-permute-done | bytes 262176 | tf_op jit(solution)/shard_map/ppermute | solution.py:240
  66.1 0.0 collective-permute-start.5
  66.1 0.0 collective-permute-done.refs_1_
  66.1 4.9 %collective-permute-done.1.refs_2_ = s16[16,2,16,256]{3,2,1,0:T(8,128)(2,1)S(1)} collective-permute-done((s16[16,2,16,256]{3,2,1,0:T(8,128)(2,1)S(1)}, s16[16,2,16,256]{3,2,1,0:T(8,128)(2,1)S(1)}, u32[]{:S(2)}, u32[]{:S(2)}) %collective-permute-start.1) | collective-permute-done | bytes 262176 | tf_op jit(solution)/shard_map/ppermute | solution.py:240
  71.0 2.6 %collective-permute-done.2.refs_3_ = s16[16,2,16,256]{3,2,1,0:T(8,128)(2,1)S(1)} collective-permute-done((s16[16,2,16,256]{3,2,1,0:T(8,128)(2,1)S(1)}, s16[16,2,16,256]{3,2,1,0:T(8,128)(2,1)S(1)}, u32[]{:S(2)}, u32[]{:S(2)}) %collective-permute-start.2) | collective-permute-done | bytes 262176 | tf_op jit(solution)/shard_map/ppermute | solution.py:240
  73.6 0.0 collective-permute-done.3.refs_5_
  73.6 0.0 collective-permute-done.5.refs_7_
  73.6 2.4 %product_one.1 = s16[16,2,16,256]{3,2,1,0:T(8,128)(2,1)S(1)} custom-call(s32[1]{0:T(128)} %bitcast.shift_ref, s16[16,2,16,256]{3,2,1,0:T(8,128)(2,1)S(1)} %get-tuple-element.14.refs_0_, s16[16,2,16,256]{3,2,1,0:T(8,128)(2,1)S(1)} %collective-permute-done.refs_1_, s16[16,2,16,256]{3,2,1,0:T(8,128)(2,1)S(1)} %collective-permute-done.1.refs_2_, ...), custom_call_target="tpu_custom_call" | custom-call | flops 805306368 | bytes 1048576 | tf_op jit(solution)/shard_map/product_one/pallas_call | solution.py:222
  76.0 16.4 %all_to_all.31.in_ref = s16[16,2,16,256]{3,2,1,0:T(8,128)(2,1)S(1)} all-to-all(s16[16,2,16,256]{3,2,1,0:T(8,128)(2,1)S(1)} %product_one.1), channel_id=1, replica_groups=mesh['row'=4,'col'=4,'pt'=16] {'pt'}, dimensions={0} | all-to-all | bytes 524288 | tf_op jit(solution)/shard_map/all_to_all | solution.py:236
  92.4 1.6 middle.1
  94.0 4.2 %all-to-all-start.4 = ((s16[16,3,16,256]{3,2,1,0:T(8,128)(2,1)}), s16[16,3,16,256]{3,2,1,0:T(8,128)(2,1)S(1)}, u32[]{:S(2)}, u32[]{:S(2)}) async-start(s16[16,3,16,256]{3,2,1,0:T(8,128)(2,1)} %middle.1), calls=%async_computation.4 | async-start | bytes 786432 | tf_op jit(solution)/shard_map/all_to_all | solution.py:236
  98.2 1.2 fusion
  99.4 2.1 %collective-permute-start.10 = (s16[16,3,16,256]{3,2,1,0:T(8,128)(2,1)S(1)}, s16[16,3,16,256]{3,2,1,0:T(8,128)(2,1)S(1)}, u32[]{:S(2)}, u32[]{:S(2)}) collective-permute-start(s16[16,3,16,256]{3,2,1,0:T(8,128)(2,1)S(1)} %get-tuple-element.11.refs_4_), channel_id=1, source_target_pairs={{0,128},{64,192},{128,0},{192,64},{1,129},{65,193},{129,1},{193,65... | collective-permute-start | bytes 1179656 | tf_op jit(solution)/shard_map/ppermute | solution.py:240
  101.5 0.0 collective-permute-start.6
  101.5 2.9 %collective-permute-start.7 = (s16[16,3,16,256]{3,2,1,0:T(8,128)(2,1)S(1)}, s16[16,3,16,256]{3,2,1,0:T(8,128)(2,1)S(1)}, u32[]{:S(2)}, u32[]{:S(2)}) collective-permute-start(s16[16,3,16,256]{3,2,1,0:T(8,128)(2,1)S(1)} %get-tuple-element.12.refs_0_), channel_id=1, source_target_pairs={{0,32},{16,48},{32,0},{48,16},{1,33},{17,49},{33,1},{49,17},{2,34}... | collective-permute-start | bytes 1179656 | tf_op jit(solution)/shard_map/ppermute | solution.py:240
  104.4 1.8 %collective-permute-start.8 = (s16[16,3,16,256]{3,2,1,0:T(8,128)(2,1)S(1)}, s16[16,3,16,256]{3,2,1,0:T(8,128)(2,1)S(1)}, u32[]{:S(2)}, u32[]{:S(2)}) collective-permute-start(s16[16,3,16,256]{3,2,1,0:T(8,128)(2,1)S(1)} %get-tuple-element.12.refs_0_), channel_id=1, source_target_pairs={{0,48},{16,32},{32,16},{48,0},{1,49},{17,33},{33,17},{49,1},{2,50}... | collective-permute-start | bytes 1179656 | tf_op jit(solution)/shard_map/ppermute | solution.py:240
  106.2 0.0 collective-permute-start.9
  106.2 6.0 %collective-permute-done.10.refs_6_ = s16[16,3,16,256]{3,2,1,0:T(8,128)(2,1)S(1)} collective-permute-done((s16[16,3,16,256]{3,2,1,0:T(8,128)(2,1)S(1)}, s16[16,3,16,256]{3,2,1,0:T(8,128)(2,1)S(1)}, u32[]{:S(2)}, u32[]{:S(2)}) %collective-permute-start.10) | collective-permute-done | bytes 393248 | tf_op jit(solution)/shard_map/ppermute | solution.py:240
  112.2 1.3 collective-permute-done.6.refs_1_
  113.5 1.1 collective-permute-start.16
  114.6 5.9 %collective-permute-done.7.refs_2_ = s16[16,3,16,256]{3,2,1,0:T(8,128)(2,1)S(1)} collective-permute-done((s16[16,3,16,256]{3,2,1,0:T(8,128)(2,1)S(1)}, s16[16,3,16,256]{3,2,1,0:T(8,128)(2,1)S(1)}, u32[]{:S(2)}, u32[]{:S(2)}) %collective-permute-start.7) | collective-permute-done | bytes 393248 | tf_op jit(solution)/shard_map/ppermute | solution.py:240
  120.5 2.6 %collective-permute-done.8.refs_3_ = s16[16,3,16,256]{3,2,1,0:T(8,128)(2,1)S(1)} collective-permute-done((s16[16,3,16,256]{3,2,1,0:T(8,128)(2,1)S(1)}, s16[16,3,16,256]{3,2,1,0:T(8,128)(2,1)S(1)}, u32[]{:S(2)}, u32[]{:S(2)}) %collective-permute-start.8) | collective-permute-done | bytes 393248 | tf_op jit(solution)/shard_map/ppermute | solution.py:240
  123.1 3.6 %product_upper.1.refs_0_ = s16[16,3,16,256]{3,2,1,0:T(8,128)(2,1)S(1)} custom-call(s32[1]{0:T(128)} %bitcast.shift_ref, s16[16,3,16,256]{3,2,1,0:T(8,128)(2,1)S(1)} %get-tuple-element.12.refs_0_, s16[16,3,16,256]{3,2,1,0:T(8,128)(2,1)S(1)} %collective-permute-done.6.refs_1_, s16[16,3,16,256]{3,2,1,0:T(8,128)(2,1)S(1)} %collective-permute-done.7.refs_2_, ...), custom_call_target="tpu_custom_call" | custom-call | flops 1207959552 | bytes 1048576 | tf_op jit(solution)/shard_map/product_upper/pallas_call | solution.py:222
  126.7 0.0 copy-start
  126.7 0.1 collective-permute-start.12
  126.8 1.7 %collective-permute-start.13 = (s16[16,3,16,256]{3,2,1,0:T(8,128)(2,1)S(1)}, s16[16,3,16,256]{3,2,1,0:T(8,128)(2,1)S(1)}, u32[]{:S(2)}, u32[]{:S(2)}) collective-permute-start(s16[16,3,16,256]{3,2,1,0:T(8,128)(2,1)S(1)} %product_upper.1.refs_0_), channel_id=1, source_target_pairs={{0,32},{16,48},{32,0},{48,16},{1,33},{17,49},{33,1},{49,17},{2,34}... | collective-permute-start | bytes 1179656 | tf_op jit(solution)/shard_map/ppermute | solution.py:240
  128.6 2.9 %collective-permute-start.14 = (s16[16,3,16,256]{3,2,1,0:T(8,128)(2,1)S(1)}, s16[16,3,16,256]{3,2,1,0:T(8,128)(2,1)S(1)}, u32[]{:S(2)}, u32[]{:S(2)}) collective-permute-start(s16[16,3,16,256]{3,2,1,0:T(8,128)(2,1)S(1)} %product_upper.1.refs_0_), channel_id=1, source_target_pairs={{0,48},{16,32},{32,16},{48,0},{1,49},{17,33},{33,17},{49,1},{2,50}... | collective-permute-start | bytes 1179656 | tf_op jit(solution)/shard_map/ppermute | solution.py:240
  131.5 0.5 collective-permute-start.17
  132.0 5.1 %collective-permute-done.12.refs_1_ = s16[16,3,16,256]{3,2,1,0:T(8,128)(2,1)S(1)} collective-permute-done((s16[16,3,16,256]{3,2,1,0:T(8,128)(2,1)S(1)}, s16[16,3,16,256]{3,2,1,0:T(8,128)(2,1)S(1)}, u32[]{:S(2)}, u32[]{:S(2)}) %collective-permute-start.12) | collective-permute-done | bytes 393248 | tf_op jit(solution)/shard_map/ppermute | solution.py:240
  137.2 3.2 %collective-permute-done.13.refs_2_ = s16[16,3,16,256]{3,2,1,0:T(8,128)(2,1)S(1)} collective-permute-done((s16[16,3,16,256]{3,2,1,0:T(8,128)(2,1)S(1)}, s16[16,3,16,256]{3,2,1,0:T(8,128)(2,1)S(1)}, u32[]{:S(2)}, u32[]{:S(2)}) %collective-permute-start.13) | collective-permute-done | bytes 393248 | tf_op jit(solution)/shard_map/ppermute | solution.py:240
  140.3 3.4 %collective-permute-done.14.refs_3_ = s16[16,3,16,256]{3,2,1,0:T(8,128)(2,1)S(1)} collective-permute-done((s16[16,3,16,256]{3,2,1,0:T(8,128)(2,1)S(1)}, s16[16,3,16,256]{3,2,1,0:T(8,128)(2,1)S(1)}, u32[]{:S(2)}, u32[]{:S(2)}) %collective-permute-start.14) | collective-permute-done | bytes 393248 | tf_op jit(solution)/shard_map/ppermute | solution.py:240
  143.7 3.7 %product_two.1 = s16[16,3,16,256]{3,2,1,0:T(8,128)(2,1)S(1)} custom-call(s32[1]{0:T(128)} %bitcast.shift_ref, s16[16,3,16,256]{3,2,1,0:T(8,128)(2,1)S(1)} %product_upper.1.refs_0_, s16[16,3,16,256]{3,2,1,0:T(8,128)(2,1)S(1)} %collective-permute-done.12.refs_1_, s16[16,3,16,256]{3,2,1,0:T(8,128)(2,1)S(1)} %collective-permute-done.13.refs_2_, ...), custom_call_target="tpu_custom_call" | custom-call | flops 1207959552 | bytes 1048576 | tf_op jit(solution)/shard_map/product_two/pallas_call | solution.py:222
  147.4 17.8 %all_to_all.32.in_ref = s16[16,3,16,256]{3,2,1,0:T(8,128)(2,1)S(1)} all-to-all(s16[16,3,16,256]{3,2,1,0:T(8,128)(2,1)S(1)} %product_two.1), channel_id=1, replica_groups=mesh['row'=4,'col'=4,'pt'=16] {'pt'}, dimensions={0} | all-to-all | bytes 786432 | tf_op jit(solution)/shard_map/all_to_all | solution.py:236
  165.2 1.9 %final.1 = f32[45,16,256]{2,1,0:T(8,128)} custom-call(bf16[720,768]{1,0:T(8,128)(2,1)S(1)} %copy-done, s16[16,3,16,256]{3,2,1,0:T(8,128)(2,1)S(1)} %all_to_all.32.in_ref), custom_call_target="tpu_custom_call" | custom-call | flops 566231040 | bytes 1048576 | tf_op jit(solution)/shard_map/final/pallas_call | solution.py:208
  (19 shorter events, 0.1 us)
Async XLA Ops:
  0.0 1.0 copy-start.1
  1.0 1.0 copy-start.2
  2.1 24.5 %copy-start.4 = (bf16[512,256]{1,0:T(8,128)(2,1)S(1)}, bf16[512,256]{1,0:T(8,128)(2,1)}, u32[]{:S(2)}) copy-start(bf16[512,256]{1,0:T(8,128)(2,1)} %constant.18.clone.table_ref) | copy-start | bytes 786436
  26.6 6.8 %copy-start.3 = (bf16[768,256]{1,0:T(8,128)(2,1)S(1)}, bf16[768,256]{1,0:T(8,128)(2,1)}, u32[]{:S(2)}) copy-start(bf16[768,256]{1,0:T(8,128)(2,1)} %constant.19.clone.table_ref) | copy-start | bytes 1179652
  28.1 20.0 %all-to-all-start.1 = ((s16[16,4,16,256]{3,2,1,0:T(8,128)(2,1)}), s16[16,4,16,256]{3,2,1,0:T(8,128)(2,1)S(1)}, u32[]{:S(2)}, u32[]{:S(2)}) async-start(s16[16,4,16,256]{3,2,1,0:T(8,128)(2,1)} %spread_one.1), calls=%async_computation.1 | async-start | bytes 1048576 | tf_op jit(solution)/shard_map/all_to_all | solution.py:236
  48.1 27.9 %all-to-all-start.2 = ((s16[16,6,16,256]{3,2,1,0:T(8,128)(2,1)}), s16[16,6,16,256]{3,2,1,0:T(8,128)(2,1)}, u32[]{:S(2)}, u32[]{:S(2)}) async-start(s16[16,6,16,256]{3,2,1,0:T(8,128)(2,1)} %spread_two.1), calls=%async_computation.2 | async-start | bytes 1572864 | tf_op jit(solution)/shard_map/all_to_all | solution.py:236
  53.3 12.8 %collective-permute-start.4 = (s16[16,2,16,256]{3,2,1,0:T(8,128)(2,1)S(1)}, s16[16,2,16,256]{3,2,1,0:T(8,128)(2,1)S(1)}, u32[]{:S(2)}, u32[]{:S(2)}) collective-permute-start(s16[16,2,16,256]{3,2,1,0:T(8,128)(2,1)S(1)} %get-tuple-element.13.refs_4_), channel_id=1, source_target_pairs={{0,128},{64,192},{128,0},{192,64},{1,129},{65,193},{129,1},{193,65... | collective-permute-start | bytes 786440 | tf_op jit(solution)/shard_map/ppermute | solution.py:240
  56.1 10.0 %collective-permute-start = (s16[16,2,16,256]{3,2,1,0:T(8,128)(2,1)S(1)}, s16[16,2,16,256]{3,2,1,0:T(8,128)(2,1)S(1)}, u32[]{:S(2)}, u32[]{:S(2)}) collective-permute-start(s16[16,2,16,256]{3,2,1,0:T(8,128)(2,1)S(1)} %get-tuple-element.14.refs_0_), channel_id=1, source_target_pairs={{0,16},{16,0},{32,48},{48,32},{1,17},{17,1},{33,49},{49,33},{2,18}... | collective-permute-start | bytes 786440 | tf_op jit(solution)/shard_map/ppermute | solution.py:240
  57.7 13.3 %collective-permute-start.1 = (s16[16,2,16,256]{3,2,1,0:T(8,128)(2,1)S(1)}, s16[16,2,16,256]{3,2,1,0:T(8,128)(2,1)S(1)}, u32[]{:S(2)}, u32[]{:S(2)}) collective-permute-start(s16[16,2,16,256]{3,2,1,0:T(8,128)(2,1)S(1)} %get-tuple-element.14.refs_0_), channel_id=1, source_target_pairs={{0,32},{16,48},{32,0},{48,16},{1,33},{17,49},{33,1},{49,17},{2,34}... | collective-permute-start | bytes 786440 | tf_op jit(solution)/shard_map/ppermute | solution.py:240
  60.6 13.0 %collective-permute-start.2 = (s16[16,2,16,256]{3,2,1,0:T(8,128)(2,1)S(1)}, s16[16,2,16,256]{3,2,1,0:T(8,128)(2,1)S(1)}, u32[]{:S(2)}, u32[]{:S(2)}) collective-permute-start(s16[16,2,16,256]{3,2,1,0:T(8,128)(2,1)S(1)} %get-tuple-element.14.refs_0_), channel_id=1, source_target_pairs={{0,48},{16,32},{32,16},{48,0},{1,49},{17,33},{33,17},{49,1},{2,50}... | collective-permute-start | bytes 786440 | tf_op jit(solution)/shard_map/ppermute | solution.py:240
  60.8 12.8 %collective-permute-start.3 = (s16[16,2,16,256]{3,2,1,0:T(8,128)(2,1)S(1)}, s16[16,2,16,256]{3,2,1,0:T(8,128)(2,1)S(1)}, u32[]{:S(2)}, u32[]{:S(2)}) collective-permute-start(s16[16,2,16,256]{3,2,1,0:T(8,128)(2,1)S(1)} %get-tuple-element.13.refs_4_), channel_id=1, source_target_pairs={{0,64},{64,0},{128,192},{192,128},{1,65},{65,1},{129,193},{193,129... | collective-permute-start | bytes 786440 | tf_op jit(solution)/shard_map/ppermute | solution.py:240
  66.1 7.5 %collective-permute-start.5 = (s16[16,2,16,256]{3,2,1,0:T(8,128)(2,1)S(1)}, s16[16,2,16,256]{3,2,1,0:T(8,128)(2,1)S(1)}, u32[]{:S(2)}, u32[]{:S(2)}) collective-permute-start(s16[16,2,16,256]{3,2,1,0:T(8,128)(2,1)S(1)} %collective-permute-done.4.refs_6_), channel_id=1, source_target_pairs={{0,64},{64,0},{128,192},{192,128},{1,65},{65,1},{129,193},{193,129... | collective-permute-start | bytes 786440 | tf_op jit(solution)/shard_map/ppermute | solution.py:240
  73.6 18.7 %copy-start.5 = (bf16[768,512]{1,0:T(8,128)(2,1)S(1)}, bf16[768,512]{1,0:T(8,128)(2,1)}, u32[]{:S(2)}) copy-start(bf16[768,512]{1,0:T(8,128)(2,1)} %constant.20.clone.table_ref) | copy-start | bytes 2359300
  94.0 19.5 %all-to-all-start.4 = ((s16[16,3,16,256]{3,2,1,0:T(8,128)(2,1)}), s16[16,3,16,256]{3,2,1,0:T(8,128)(2,1)S(1)}, u32[]{:S(2)}, u32[]{:S(2)}) async-start(s16[16,3,16,256]{3,2,1,0:T(8,128)(2,1)} %middle.1), calls=%async_computation.4 | async-start | bytes 786432 | tf_op jit(solution)/shard_map/all_to_all | solution.py:236
  99.4 12.9 %collective-permute-start.10 = (s16[16,3,16,256]{3,2,1,0:T(8,128)(2,1)S(1)}, s16[16,3,16,256]{3,2,1,0:T(8,128)(2,1)S(1)}, u32[]{:S(2)}, u32[]{:S(2)}) collective-permute-start(s16[16,3,16,256]{3,2,1,0:T(8,128)(2,1)S(1)} %get-tuple-element.11.refs_4_), channel_id=1, source_target_pairs={{0,128},{64,192},{128,0},{192,64},{1,129},{65,193},{129,1},{193,65... | collective-permute-start | bytes 1179656 | tf_op jit(solution)/shard_map/ppermute | solution.py:240
  101.5 12.0 %collective-permute-start.6 = (s16[16,3,16,256]{3,2,1,0:T(8,128)(2,1)S(1)}, s16[16,3,16,256]{3,2,1,0:T(8,128)(2,1)S(1)}, u32[]{:S(2)}, u32[]{:S(2)}) collective-permute-start(s16[16,3,16,256]{3,2,1,0:T(8,128)(2,1)S(1)} %get-tuple-element.12.refs_0_), channel_id=1, source_target_pairs={{0,16},{16,0},{32,48},{48,32},{1,17},{17,1},{33,49},{49,33},{2,18}... | collective-permute-start | bytes 1179656 | tf_op jit(solution)/shard_map/ppermute | solution.py:240
  101.5 19.0 %collective-permute-start.7 = (s16[16,3,16,256]{3,2,1,0:T(8,128)(2,1)S(1)}, s16[16,3,16,256]{3,2,1,0:T(8,128)(2,1)S(1)}, u32[]{:S(2)}, u32[]{:S(2)}) collective-permute-start(s16[16,3,16,256]{3,2,1,0:T(8,128)(2,1)S(1)} %get-tuple-element.12.refs_0_), channel_id=1, source_target_pairs={{0,32},{16,48},{32,0},{48,16},{1,33},{17,49},{33,1},{49,17},{2,34}... | collective-permute-start | bytes 1179656 | tf_op jit(solution)/shard_map/ppermute | solution.py:240
  104.4 18.7 %collective-permute-start.8 = (s16[16,3,16,256]{3,2,1,0:T(8,128)(2,1)S(1)}, s16[16,3,16,256]{3,2,1,0:T(8,128)(2,1)S(1)}, u32[]{:S(2)}, u32[]{:S(2)}) collective-permute-start(s16[16,3,16,256]{3,2,1,0:T(8,128)(2,1)S(1)} %get-tuple-element.12.refs_0_), channel_id=1, source_target_pairs={{0,48},{16,32},{32,16},{48,0},{1,49},{17,33},{33,17},{49,1},{2,50}... | collective-permute-start | bytes 1179656 | tf_op jit(solution)/shard_map/ppermute | solution.py:240
  106.2 16.9 %collective-permute-start.9 = (s16[16,3,16,256]{3,2,1,0:T(8,128)(2,1)S(1)}, s16[16,3,16,256]{3,2,1,0:T(8,128)(2,1)S(1)}, u32[]{:S(2)}, u32[]{:S(2)}) collective-permute-start(s16[16,3,16,256]{3,2,1,0:T(8,128)(2,1)S(1)} %get-tuple-element.11.refs_4_), channel_id=1, source_target_pairs={{0,64},{64,0},{128,192},{192,128},{1,65},{65,1},{129,193},{193,129... | collective-permute-start | bytes 1179656 | tf_op jit(solution)/shard_map/ppermute | solution.py:240
  112.2 10.8 %collective-permute-start.11 = (s16[16,3,16,256]{3,2,1,0:T(8,128)(2,1)S(1)}, s16[16,3,16,256]{3,2,1,0:T(8,128)(2,1)S(1)}, u32[]{:S(2)}, u32[]{:S(2)}) collective-permute-start(s16[16,3,16,256]{3,2,1,0:T(8,128)(2,1)S(1)} %collective-permute-done.10.refs_6_), channel_id=1, source_target_pairs={{0,64},{64,0},{128,192},{192,128},{1,65},{65,1},{129,193},{193,129... | collective-permute-start | bytes 1179656 | tf_op jit(solution)/shard_map/ppermute | solution.py:240
  113.5 18.0 %collective-permute-start.16 = (s16[16,3,16,256]{3,2,1,0:T(8,128)(2,1)S(1)}, s16[16,3,16,256]{3,2,1,0:T(8,128)(2,1)S(1)}, u32[]{:S(2)}, u32[]{:S(2)}) collective-permute-start(s16[16,3,16,256]{3,2,1,0:T(8,128)(2,1)S(1)} %all-to-all-done.4.refs_4_), channel_id=1, source_target_pairs={{0,128},{64,192},{128,0},{192,64},{1,129},{65,193},{129,1},{193,65... | collective-permute-start | bytes 1179656 | tf_op jit(solution)/shard_map/ppermute | solution.py:240
  126.7 38.5 %copy-start = (bf16[720,768]{1,0:T(8,128)(2,1)S(1)}, bf16[720,768]{1,0:T(8,128)(2,1)}, u32[]{:S(2)}) copy-start(bf16[720,768]{1,0:T(8,128)(2,1)} %constant.21.clone.table_ref) | copy-start | bytes 3317764
  126.7 10.4 %collective-permute-start.12 = (s16[16,3,16,256]{3,2,1,0:T(8,128)(2,1)S(1)}, s16[16,3,16,256]{3,2,1,0:T(8,128)(2,1)S(1)}, u32[]{:S(2)}, u32[]{:S(2)}) collective-permute-start(s16[16,3,16,256]{3,2,1,0:T(8,128)(2,1)S(1)} %product_upper.1.refs_0_), channel_id=1, source_target_pairs={{0,16},{16,0},{32,48},{48,32},{1,17},{17,1},{33,49},{49,33},{2,18}... | collective-permute-start | bytes 1179656 | tf_op jit(solution)/shard_map/ppermute | solution.py:240
  126.8 13.5 %collective-permute-start.13 = (s16[16,3,16,256]{3,2,1,0:T(8,128)(2,1)S(1)}, s16[16,3,16,256]{3,2,1,0:T(8,128)(2,1)S(1)}, u32[]{:S(2)}, u32[]{:S(2)}) collective-permute-start(s16[16,3,16,256]{3,2,1,0:T(8,128)(2,1)S(1)} %product_upper.1.refs_0_), channel_id=1, source_target_pairs={{0,32},{16,48},{32,0},{48,16},{1,33},{17,49},{33,1},{49,17},{2,34}... | collective-permute-start | bytes 1179656 | tf_op jit(solution)/shard_map/ppermute | solution.py:240
  128.6 15.2 %collective-permute-start.14 = (s16[16,3,16,256]{3,2,1,0:T(8,128)(2,1)S(1)}, s16[16,3,16,256]{3,2,1,0:T(8,128)(2,1)S(1)}, u32[]{:S(2)}, u32[]{:S(2)}) collective-permute-start(s16[16,3,16,256]{3,2,1,0:T(8,128)(2,1)S(1)} %product_upper.1.refs_0_), channel_id=1, source_target_pairs={{0,48},{16,32},{32,16},{48,0},{1,49},{17,33},{33,17},{49,1},{2,50}... | collective-permute-start | bytes 1179656 | tf_op jit(solution)/shard_map/ppermute | solution.py:240
  131.5 12.2 %collective-permute-start.15 = (s16[16,3,16,256]{3,2,1,0:T(8,128)(2,1)S(1)}, s16[16,3,16,256]{3,2,1,0:T(8,128)(2,1)S(1)}, u32[]{:S(2)}, u32[]{:S(2)}) collective-permute-start(s16[16,3,16,256]{3,2,1,0:T(8,128)(2,1)S(1)} %all-to-all-done.4.refs_4_), channel_id=1, source_target_pairs={{0,64},{64,0},{128,192},{192,128},{1,65},{65,1},{129,193},{193,129... | collective-permute-start | bytes 1179656 | tf_op jit(solution)/shard_map/ppermute | solution.py:240
  131.5 12.2 %collective-permute-start.17 = (s16[16,3,16,256]{3,2,1,0:T(8,128)(2,1)S(1)}, s16[16,3,16,256]{3,2,1,0:T(8,128)(2,1)S(1)}, u32[]{:S(2)}, u32[]{:S(2)}) collective-permute-start(s16[16,3,16,256]{3,2,1,0:T(8,128)(2,1)S(1)} %collective-permute-done.16.refs_6_), channel_id=1, source_target_pairs={{0,64},{64,0},{128,192},{192,128},{1,65},{65,1},{129,193},{193,129... | collective-permute-start | bytes 1179656 | tf_op jit(solution)/shard_map/ppermute | solution.py:240
